TPU v7x, 32 devices: a whole 2x2x4 slice. The times are simulated.
32 devices in a mesh: hist: 4 (over z), rows: 2 (over y), dom: 4 (over x, core).
Axes of the slice: x: 2, y: 2, z: 4, core: 2. Of those that a mesh axis runs over, the one named last changes fastest.
Arguments:
- row_index: int32 [4, 32768], P(None, ('hist', 'rows', 'dom')), may hold values from 0 to 510
- col_index: int32 [4, 32768], P(None, ('hist', 'rows', 'dom')), may hold values from 0 to 510
- bin_index: int32 [4, 32768], P(None, ('hist', 'rows', 'dom')), may hold values from 0 to 255
- charge: bfloat16 [32768], P(('hist', 'rows', 'dom')), may hold values from 0.5 to 2
- momentum: float32 [2, 32768], P(None, ('hist', 'rows', 'dom')), may hold values from -6 to 6
- history: bfloat16 [32, 512, 512], P('hist', 'rows'), may hold values from 0 to 2
- kernel_cols: bfloat16 [32, 512, 512], P('hist', 'dom'), may hold values from -0.25 to 0.25
- kernel_rows: bfloat16 [32, 512, 2, 512], P('hist', 'rows'), may hold values from -0.046875 to 0.046875
Outputs:
- momentum_out: float32 [2, 32768], P(None, ('hist', 'rows', 'dom'))
- history_out: bfloat16 [32, 512, 512], P('hist', 'rows')
All inputs are finite; a program needn't handle non-finite values.
Results may differ from a plain program's by a relative error of at most 0.0024.
Values may be sent and summed in bfloat16 or wider, within the bound.
A program may use at most 64 MiB of HBM per device.

v0:
```python
import functools
import jax
import jax.numpy as jnp
from jax import lax
from jax.experimental import pallas as pl
from jax.experimental.pallas import tpu as pltpu
from jax.sharding import PartitionSpec as P

NG = 512
BINS = 16
STEPS = 4
CORES = 2
HALVES = 4
kick_scale = 0.5

MESH = pl.DeviceIdType.MESH
VM = pl.BlockSpec(memory_space=pltpu.VMEM)
NT = (((1,), (1,)), ((), ()))


def place():
    return lax.axis_index("hist"), lax.axis_index("rows"), lax.axis_index("dom")


def hat(extent, whole, near, far):
    kind = jnp.bfloat16
    places = lax.broadcasted_iota(jnp.int32, (extent, whole.shape[1]), 0).astype(kind)
    first = whole.astype(kind)
    return jnp.where(places == first, near.astype(kind),
                     jnp.where(places == first + kind(1.0), far.astype(kind), kind(0.0)))


def plane_peer(rows, dom, shift):
    h, r, d = place()
    other = lax.rem(r * dom + d + shift, rows * dom)
    return other, (h, other // dom, lax.rem(other, dom))


def drain(ref, sem):
    pltpu.make_async_copy(ref, ref, sem).wait()


def inside(index, count):
    return jnp.logical_and(index >= 0, index < count)


def kernel(hist, rows, dom, row_ref, col_ref, bin_ref, charge_ref, momentum, old_ref, cols_ref, rows_ref,
           out, newest, places, charge_in, start, spots, charges, base, frac, lefts, rights, dens, summed, arrived, gath, grids, cols, raw, turned, total,
           parts, got, mine, from_low, from_high, to_high, to_low, table, kicks, got_kicks, load, sent, once,
           sem_a, sem_h, sem_c, sem_x, sem_g, sem_y, sem_u, sem_d):
    h, r, d = place()
    n = rows * dom
    lags, width, _ = cols.shape
    band = old_ref.shape[1]
    keep = lefts.shape[0] == n
    piece = NG // rows
    size = width // HALVES
    kind = parts.dtype
    chips = dom // CORES
    up, down = (h + 1, r, d), (h - 1, r, d)
    levels = (hist - 1).bit_length()
    sums = [jnp.logical_and(lax.rem(h, 2 << a) == 0, h + (1 << a) < hist) for a in range(levels)]
    gives = [lax.rem(h, 2 << a) == 1 << a for a in range(levels)]
    rank = sum(jnp.where(lax.rem(h, 1 << a) == 0, 1, 0) for a in range(1, levels + 1))
    partner = (h, r, d + 1 - 2 * lax.rem(d, CORES))
    across = [(h, r, lax.rem(d + CORES * j, dom)) for j in range(1, chips)]
    is_first, is_last = h == 0, h == hist - 1
    below, above = jnp.logical_not(is_last), jnp.logical_not(is_first)
    inner = jnp.logical_and(below, above)

    loads = (pltpu.make_async_copy(old_ref, grids.at[pl.ds(STEPS, lags)], load.at[0]),
             pltpu.make_async_copy(cols_ref, cols, load.at[1]),
             pltpu.make_async_copy(rows_ref, raw, load.at[2]))
    small = [pltpu.make_async_copy(src, places.at[i], load.at[3])
             for i, src in enumerate((row_ref, col_ref, bin_ref))]
    small += [pltpu.make_async_copy(charge_ref, charge_in, load.at[4]),
              pltpu.make_async_copy(momentum, start, load.at[5])]
    for copy in small:
        copy.start()
    barrier = pltpu.get_barrier_semaphore()

    @pl.when(below)
    def _():
        pl.semaphore_signal(barrier, inc=1, device_id=up, device_id_type=MESH)

    @pl.when(above)
    def _():
        pl.semaphore_signal(barrier, inc=1, device_id=down, device_id_type=MESH)

    for shift in range(1, n):
        pl.semaphore_signal(barrier, inc=1, device_id=plane_peer(rows, dom, shift)[1], device_id_type=MESH)
    count = n - 1 + jnp.where(is_first, 0, 1) + jnp.where(is_last, 0, 1)
    for a in range(1, levels):
        count += jnp.where(jnp.logical_or(sums[a], gives[a]), 1, 0)

        @pl.when(sums[a])
        def _():
            pl.semaphore_signal(barrier, inc=1, device_id=(h + (1 << a), r, d), device_id_type=MESH)

        @pl.when(gives[a])
        def _():
            pl.semaphore_signal(barrier, inc=1, device_id=(h - (1 << a), r, d), device_id_type=MESH)

    for copy in loads:
        copy.start()
    drain(places, load.at[3])
    for copy in small[3:]:
        copy.wait()
    bins = places[2]
    row_bin = bins // BINS
    down_at = places[0].astype(jnp.float32) + (row_bin.astype(jnp.float32) + 0.5) / BINS
    over_at = places[1].astype(jnp.float32) + ((bins - row_bin * BINS).astype(jnp.float32) + 0.5) / BINS
    for s in range(STEPS):
        spots[0, s, 0:1, :] = down_at[s:s + 1]
        spots[0, s, 1:2, :] = over_at[s:s + 1]
    charges[0] = charge_in[...].astype(jnp.float32).reshape(1, -1)
    pl.semaphore_wait(barrier, count)

    def remote(src, dst, s_sem, r_sem, device):
        return pltpu.make_async_remote_copy(src_ref=src, dst_ref=dst, send_sem=s_sem, recv_sem=r_sem,
                                            device_id=device, device_id_type=MESH)

    def spot_copy(shift, s):
        return remote(spots.at[0, s], spots.at[shift, s], sent.at[0], sem_a.at[s],
                      plane_peer(rows, dom, shift)[1])

    def charge_copy(shift):
        return remote(charges.at[0], charges.at[shift], sent.at[1], once.at[0], plane_peer(rows, dom, shift)[1])

    def tail_copy(s):
        columns = pl.ds(pl.multiple_of(d * width, width), width)
        return remote(old_ref.at[lags - 1 - s, :, columns], gath.at[d, s], sent.at[2], sem_h.at[s], up)

    def tree_copy(s, a):
        return remote(summed.at[s], arrived.at[s, a], sent.at[3], sem_c.at[s, a], (h - (1 << a), r, d))

    def cross_copy(s, j):
        return remote(gath.at[d, s], gath.at[d, s], sent.at[4], sem_x.at[s, j - 1], across[j - 1])

    def partner_copy(s):
        return remote(gath.at[d, s], gath.at[d, s], sent.at[4], sem_g.at[s], partner)

    def forward_copy(s, j):
        other = lax.rem(d + CORES * (chips - j), dom)
        return remote(gath.at[other, s], gath.at[other, s], sent.at[4], sem_g.at[s], partner)

    def span(c):
        return pl.ds(pl.multiple_of(c * size, size), size)

    def row_copy(c, j):
        other = lax.rem(r + j, rows)
        return remote(parts.at[other, span(c)], got.at[j - 1, span(c)], sent.at[5], sem_y.at[c, j - 1],
                      (h, other, d))

    def up_copy(c):
        return remote(to_high.at[span(c)], from_low.at[span(c)], sent.at[6], sem_u.at[c], up)

    def down_copy(c):
        return remote(to_low.at[span(c)], from_high.at[span(c)], sent.at[7], sem_d.at[c], down)

    def kick_copy(k):
        return remote(kicks.at[k], got_kicks.at[k], sent.at[8], once.at[1], plane_peer(rows, dom, n - k)[1])

    def fresh(s):
        return pltpu.make_async_copy(grids.at[STEPS - 1 - s], newest.at[STEPS - 1 - s], load.at[6])

    for s in range(STEPS):
        for shift in range(1, n):
            spot_copy(shift, s).start()
            if s == 0:
                charge_copy(shift).start()

    @pl.when(below)
    def _():
        for s in range(STEPS):
            tail_copy(s).start()

    total[...] = jnp.zeros_like(total)
    dens[...] = jnp.zeros_like(dens)
    kicks[...] = jnp.zeros_like(kicks)
    for copy in loads:
        copy.wait()

    def add_field(weights, mixed, where):
        for comp in range(2):
            total[comp, where] += jnp.dot(mixed, weights[comp], preferred_element_type=jnp.float32)

    def products(k, weights, begin, steps, first=0):
        window = grids[pl.ds(begin, steps)].reshape(steps * band, NG)
        mixed = lax.dot_general(cols[k], window, NT, preferred_element_type=jnp.float32).astype(kind)
        stacked = jnp.concatenate(
            [mixed[:, (steps - 1 - s) * band:(steps - s) * band] for s in range(steps)], axis=0)
        add_field(weights, stacked, pl.ds(first * width, steps * width))

    def whole_lag(k):
        products(k, pltpu.einshape("acb->cab", raw[k]), k, STEPS)

    ahead = max(0, lags - STEPS - 2)

    def lag(k, carry):
        whole_lag(k)
        return carry

    lax.fori_loop(STEPS, STEPS + ahead, lag, 0)
    turned[0] = pltpu.einshape("acb->cab", raw[0])
    for k in range(1, STEPS):
        turned[k] = pltpu.einshape("acb->cab", raw[k])
        products(k, turned[k], STEPS, k)

    side = lax.broadcasted_iota(jnp.int32, (2, 1), 0)
    corner = jnp.where(side == 0, r * band, d * width).astype(jnp.float32)

    def settle(k, s):
        value = spots[k, s]
        floor = jnp.floor(value)
        base[k, s] = floor - corner
        frac[k, s] = value - floor

    def hats(k, s):
        whole, part = base[k, s], frac[k, s]
        left = hat(band, whole[0:1], 1.0 - part[0:1], part[0:1])
        right = hat(width, whole[1:2], 1.0 - part[1:2], part[1:2])
        return left, right

    def deposit(s):
        drain(spots.at[pl.ds(1, n - 1), s], sem_a.at[s])

        @pl.when(s == 0)
        def _():
            drain(charges.at[pl.ds(1, n - 1)], once.at[0])

        def arrive(k, carry):
            settle(k, s)
            return carry

        lax.fori_loop(0, n, arrive, 0, unroll=8)

        def block(k, carry):
            left, right = hats(k, s)
            if keep:
                lefts[k, s] = left
                rights[k, s] = right
            left = left * charges[k].astype(kind)
            dens[s] += lax.dot_general(left, right, NT, preferred_element_type=jnp.float32)
            return carry

        lax.fori_loop(0, n, block, 0, unroll=8)

    def relay(s):
        for a in range(levels):
            @pl.when(sums[a])
            def _():
                tree_copy(s, a).wait_recv()
                dens[s] += arrived[s, a].astype(jnp.float32)

        @pl.when(is_first)
        def _():
            gath[d, s] = dens[s].astype(kind)

        @pl.when(above)
        def _():
            summed[s] = dens[s].astype(kind)

        for a in range(levels):
            @pl.when(gives[a])
            def _():
                tree_copy(s, a).start()

    def gather(s):
        @pl.when(above)
        def _():
            tail_copy(s).wait_recv()

        for j in range(1, chips):
            cross_copy(s, j).start()
        partner_copy(s).start()

    def forward(s):
        for j in range(1, chips):
            cross_copy(s, j).wait_recv()
            forward_copy(s, j).start()

    def assemble(s):
        drain(gath.at[pl.ds(0, chips), s], sem_g.at[s])
        grids[STEPS - 1 - s] = jnp.concatenate([gath[e, s] for e in range(dom)], axis=1)
        fresh(s).start()

    def strip(s):
        return pl.ds(pl.multiple_of(s * width, width), width)

    def post(s):
        where = strip(s)
        for q in range(rows):
            block = jnp.concatenate([total[comp, where, q * piece:(q + 1) * piece] for comp in range(2)], axis=1)

            @pl.when(r == q)
            def _():
                mine[where] = block

            @pl.when(r != q)
            def _():
                parts[q, where] = block.astype(kind)

        for half in range(HALVES):
            for j in range(1, rows):
                row_copy(s * HALVES + half, j).start()

    def add_late(k, s):
        mixed = lax.dot_general(cols[k], grids[STEPS - 1 - s], NT, preferred_element_type=jnp.float32).astype(kind)
        add_field(turned[k], mixed, strip(s + k))

    def late(s):
        assemble(s)
        add_late(0, s)
        post(s)

    def late_more(s):
        def add(k, carry):
            add_late(k, s)
            return carry

        lax.fori_loop(1, STEPS - s, add, 0)

    def late_all(_):
        for s in range(STEPS):
            assemble(s)
        for k in range(STEPS):
            products(k, turned[k], k, STEPS - k, k)
        for s in range(STEPS):
            post(s)

    def spread(c):
        value = mine[span(c)]
        for j in range(1, rows):
            row_copy(c, j).wait_recv()
            value += got[j - 1, span(c)].astype(jnp.float32)
        mine[span(c)] = value

        @pl.when(is_first)
        def _():
            to_high[span(c)] = value.astype(kind)
            up_copy(c).start()

        @pl.when(is_last)
        def _():
            to_low[span(c)] = value.astype(kind)
            down_copy(c).start()

    def rise(c):
        up_copy(c).wait_recv()

        @pl.when(inner)
        def _():
            to_high[span(c)] = (mine[span(c)] + from_low[span(c)].astype(jnp.float32)).astype(kind)
            up_copy(c).start()

    def sink(c):
        down_copy(c).wait_recv()

        @pl.when(inner)
        def _():
            to_low[span(c)] = (mine[span(c)] + from_high[span(c)].astype(jnp.float32)).astype(kind)
            down_copy(c).start()

    def side_hat(k, s, c):
        tall = 2 * size
        whole, part = base[k, s], frac[k, s]
        shift = ((lax.rem(c, HALVES) // 2) * tall).astype(jnp.float32)
        return hat(tall, whole[1:2] - shift, 1.0 - part[1:2], part[1:2]).astype(jnp.float32)

    def kick(c):
        s, part = c // HALVES, lax.rem(c, 2)
        share, tall = n // 2, 2 * size
        rows_c = pl.ds(pl.multiple_of((c // 2) * tall, tall), tall)
        cols_c = pl.ds(pl.multiple_of((lax.rem(c, HALVES) // 2) * tall, tall), tall)

        @pl.when(part == 0)
        def _():
            value = mine[rows_c]
            value += jnp.where(above, from_low[rows_c].astype(jnp.float32), 0.0)
            value += jnp.where(below, from_high[rows_c].astype(jnp.float32), 0.0)
            table[0:tall] = value[:, :band].astype(kind)
            table[tall:] = value[:, band:].astype(kind)

        def block(i, carry):
            k = part * share + i
            left = lefts[k, s] if keep else hats(k, s)[0]
            right = rights[k, s, cols_c].astype(jnp.float32) if keep else side_hat(k, s, c)
            along = jnp.dot(table[...], left, preferred_element_type=jnp.float32)
            for comp in range(2):
                kicks[k, comp:comp + 1, :] += jnp.sum(
                    along[comp * tall:(comp + 1) * tall] * right, axis=0, keepdims=True)
            return carry

        lax.fori_loop(0, share, block, 0, unroll=4)

    early, level, pieces = STEPS + 1, 2 * levels, STEPS * HALVES
    begin, hop = HALVES * (early + 1), HALVES
    zero = HALVES * (level + 3) + HALVES // 2
    zero = HALVES * (level + 3) + 2
    row_lag = jnp.where(is_first, zero, begin)
    rise_lag = begin + 8 + 5 * (h - 1)
    sink_lag = jnp.where(is_first, zero + 12, begin + 4 + 4 * (hist - 2 - h))
    kick_lag = jnp.where(is_first, sink_lag, jnp.where(is_last, rise_lag, jnp.maximum(rise_lag, sink_lag))) + 1
    last = max(zero + 12, begin + 8 + 5 * (hist - 2), begin + max(8 + 5 * (hist - 3), 4 + 4 * (hist - 3))) + 1

    def at(index, action, count=STEPS):
        @pl.when(inside(index, count))
        def _():
            action(index)

    def tick(t, carry):
        at(t, deposit)

        @pl.when(is_first)
        def _():
            at(t - level - 2, late)

        at(t - 2 * rank, relay)
        at(jnp.where(is_first, t - level, 2 * t), gather)

        @pl.when(above)
        def _():
            at(2 * t + 1, gather)
            at(t - early, late_all, 1)

        def turn(i, carry):
            c = HALVES * t + i
            at(c - row_lag, spread, pieces)

            @pl.when(jnp.logical_and(below, sink_first))
            def _():
                at(c - sink_lag, sink, pieces)

            @pl.when(above)
            def _():
                at(c - rise_lag, rise, pieces)

            @pl.when(jnp.logical_not(sink_first))
            def _():
                at(c - sink_lag, sink, pieces)

            at(c - kick_lag, kick, pieces)
            return carry

        @pl.when(t >= min(early + 1, level + 3))
        def _():
            lax.fori_loop(0, HALVES, turn, 0)

        at(jnp.where(is_first, t - level - 1, 2 * (t - STEPS + 1)), forward)

        @pl.when(above)
        def _():
            at(2 * (t - STEPS + 1) + 1, forward)

        @pl.when(is_first)
        def _():
            at(t - level - 2, late_more)

        spare = STEPS + ahead + jnp.where(is_first, t - STEPS, t - STEPS + 1)

        @pl.when(jnp.logical_and(spare >= STEPS + ahead, spare < lags))
        def _():
            whole_lag(spare)

        return carry

    sink_first = h > 0
    lax.fori_loop(0, -(-(last + pieces) // HALVES), tick, 0)

    for k in range(1, n):
        kick_copy(k).start()
    drain(spots.at[pl.ds(0, n - 1)], sent.at[0])
    drain(charges.at[pl.ds(0, n - 1)], sent.at[1])
    drain(gath.at[pl.ds(0, 2 * chips - 1)], sent.at[4])
    drain(got, sent.at[5])
    pltpu.make_async_copy(grids.at[pl.ds(0, STEPS)], newest, load.at[6]).wait()

    @pl.when(above)
    def _():
        drain(summed, sent.at[3])
        drain(from_high, sent.at[7])

    @pl.when(below)
    def _():
        drain(gath.at[0], sent.at[2])
        drain(from_low, sent.at[6])

    drain(kicks.at[pl.ds(0, n - 1)], sent.at[8])
    drain(got_kicks.at[pl.ds(1, n - 1)], once.at[1])
    sum_all = kicks[0]
    for k in range(1, n):
        sum_all = sum_all + got_kicks[k]
    out[...] = start[...] + kick_scale * sum_all


def finish_kernel(moved, newest, old, out, history, writes):
    fresh, kept = newest.shape[0], history.shape[0] - newest.shape[0]
    stores = (pltpu.make_async_copy(newest, history.at[pl.ds(0, fresh)], writes.at[0]),
              pltpu.make_async_copy(old.at[pl.ds(0, kept)], history.at[pl.ds(fresh, kept)], writes.at[1]),
              pltpu.make_async_copy(moved, out, writes.at[2]))
    for copy in stores:
        copy.start()
    for copy in stores:
        copy.wait()


def finish(moved, newest, history):
    anywhere = pl.BlockSpec(memory_space=pl.ANY)
    return pl.pallas_call(
        finish_kernel,
        out_shape=(jax.ShapeDtypeStruct(moved.shape, moved.dtype), jax.ShapeDtypeStruct(history.shape, history.dtype)),
        in_specs=[VM] * 3, out_specs=(anywhere, anywhere),
        scratch_shapes=[pltpu.SemaphoreType.DMA((3,))],
        compiler_params=pltpu.CompilerParams(vmem_limit_bytes=8 * 2 ** 20),
    )(moved, newest, history)


def local(hist, rows, dom, row_index, col_index, bin_index, charge, momentum, history, kernel_cols, kernel_rows):
    lags, band, _ = history.shape
    width = kernel_cols.shape[1]
    own = row_index.shape[1]
    n = rows * dom
    chips, levels = dom // CORES, (hist - 1).bit_length()
    tall, wide = STEPS * width, 2 * NG // rows
    count = STEPS * HALVES
    kind, wider = jnp.bfloat16, jnp.float32
    dma, vmem = pltpu.SemaphoreType.DMA, pltpu.VMEM
    anywhere = pl.BlockSpec(memory_space=pl.ANY)
    tile = (STEPS, band, width)
    flat = vmem((tall, wide), kind)
    each = vmem((n,) + momentum.shape, wider)
    kept = n if n * STEPS * (band + width) * own * 2 <= 32 * 2 ** 20 else 1
    steps = (STEPS, own)
    spot = vmem((n, STEPS, 2, own), wider)
    moved, newest = pl.pallas_call(
        functools.partial(kernel, hist, rows, dom),
        out_shape=(jax.ShapeDtypeStruct(momentum.shape, wider),
                   jax.ShapeDtypeStruct((STEPS, band, NG), kind)),
        in_specs=[pl.BlockSpec(memory_space=pltpu.HBM)] * 8, out_specs=(VM, anywhere),
        scratch_shapes=[vmem((3,) + steps, jnp.int32), vmem((own,), kind),
                        vmem(momentum.shape, wider), spot, vmem((n, 1, own), wider), spot, spot,
                        vmem((kept, STEPS, band, own), kind), vmem((kept, STEPS, width, own), kind),
                        vmem(tile, wider), vmem(tile, kind), vmem((STEPS, levels) + tile[1:], kind),
                        vmem((dom,) + tile, kind), vmem((lags + STEPS, band, NG), kind),
                        vmem(kernel_cols.shape, kind), vmem(kernel_rows.shape, kind),
                        vmem((STEPS, 2, band, NG), kind), vmem((2, tall, NG), wider),
                        vmem((rows, tall, wide), kind), vmem((rows - 1, tall, wide), kind), vmem((tall, wide), wider),
                        flat, flat, flat, flat, vmem((4 * width // HALVES, band), kind), each, each, dma((7,)), dma((9,)), dma((2,)), dma((STEPS,)),
                        dma((STEPS,)), dma((STEPS, levels)), dma((STEPS, chips - 1)), dma((STEPS,)),
                        dma((count, rows - 1)), dma((count,)), dma((count,))],
        compiler_params=pltpu.CompilerParams(collective_id=1, has_side_effects=True,
                                             vmem_limit_bytes=50 * 2 ** 20),
    )(*(pltpu.with_memory_space_constraint(x, pltpu.HBM) for x in (
        row_index, col_index, bin_index, charge, momentum, history, kernel_cols, kernel_rows)))
    return finish(moved, newest, history)


def solution(mesh):
    spread = ("hist", "rows", "dom")
    in_specs = (P(None, spread), P(None, spread), P(None, spread), P(spread), P(None, spread),
                P("hist", "rows", None), P("hist", "dom", None), P("hist", "rows", None, None))
    out_specs = (P(None, spread), P("hist", "rows", None))
    sizes = mesh.shape
    body = functools.partial(local, sizes["hist"], sizes["rows"], sizes["dom"])
    return jax.shard_map(body, mesh=mesh, in_specs=in_specs, out_specs=out_specs, check_vma=False)
```

profile of v0, /device:TPU:0, one launch (start us, length us, event | category | flops | bytes accessed | tf_op | source)
XLA Modules:
  0.0 53.6 jit_solution(14189355806673151128)
XLA Ops:
  0.6 0.0 copy-start
  0.6 51.6 %shard_map.95 = (f32[2,1024]{1,0:T(2,128)S(1)}, bf16[4,256,512]{2,1,0:T(8,128)(2,1)S(1)}) custom-call(s32[4,1024]{1,0:T(4,128)} %row_ref.1, s32[4,1024]{1,0:T(4,128)} %col_ref.1, s32[4,1024]{1,0:T(4,128)} %bin_ref.1, bf16[1024]{0:T(1024)(128)(2,1)} %charge_ref.1, f32[2,1024]{1,0:T(2,128)} %momentum.1, bf16[8,256,512]{2,1,0:T(8,128)(2,1)} %old.1, ...), custom_call_target="tpu_custom_call" | custom-call | tf_op jit(solution)/shard_map/pallas_call | solution.py:536
  52.2 0.0 copy-done
  52.2 1.3 %shard_map.96 = (f32[2,1024]{1,0:T(2,128)}, bf16[8,256,512]{2,1,0:T(8,128)(2,1)}) custom-call(f32[2,1024]{1,0:T(2,128)S(1)} %get-tuple-element.4.moved, bf16[4,256,512]{2,1,0:T(8,128)(2,1)S(1)} %get-tuple-element.5.newest, bf16[8,256,512]{2,1,0:T(8,128)(2,1)S(1)} %copy-done), custom_call_target="tpu_custom_call" | custom-call | tf_op jit(solution)/shard_map/pallas_call | solution.py:510
Async XLA Ops:
  0.6 51.6 %copy-start = (bf16[8,256,512]{2,1,0:T(8,128)(2,1)S(1)}, bf16[8,256,512]{2,1,0:T(8,128)(2,1)}, u32[]{:S(2)}) copy-start(bf16[8,256,512]{2,1,0:T(8,128)(2,1)} %old.1) | copy-start | bytes 6291460
where the time goes:
time: 53.8 us; the launch traced here: 53.6 us
  Pallas kernels  52.9 us (98%)
  between operations  0.66 us (1%)
    pallas_call x1, Pallas kernels, local(): pl.pallas_call(functools.partial(kernel, hist, rows, dom), out_shape=(jax...  51.6 us
    pallas_call x1, Pallas kernels, finish(): pl.pallas_call(finish_kernel, out_shape=(jax.ShapeDtypeStruct(moved.shape...  1.35 us

commit v1 on v0

--- a/solution.py
+++ b/solution.py
@@ -399,8 +399,8 @@
     zero = HALVES * (level + 3) + HALVES // 2
     zero = HALVES * (level + 3) + 2
     row_lag = jnp.where(is_first, zero, begin)
-    rise_lag = begin + 8 + 5 * (h - 1)
-    sink_lag = jnp.where(is_first, zero + 12, begin + 4 + 4 * (hist - 2 - h))
+    rise_lag = begin + 7 + 5 * (h - 1)
+    sink_lag = jnp.where(is_first, zero + 11, begin + 4 + 4 * (hist - 2 - h))
     kick_lag = jnp.where(is_first, sink_lag, jnp.where(is_last, rise_lag, jnp.maximum(rise_lag, sink_lag))) + 1
     last = max(zero + 12, begin + 8 + 5 * (hist - 2), begin + max(8 + 5 * (hist - 3), 4 + 4 * (hist - 3))) + 1
 

time: 53.8 us -> 54.2 us (level)
  no operation moved by 1% of the time
where the time goes in v1:
time: 54.2 us; the launch traced here: 54 us
  Pallas kernels  53.4 us (99%)
  between operations  0.66 us (1%)
    pallas_call x1, Pallas kernels, local(): pl.pallas_call(functools.partial(kernel, hist, rows, dom), out_shape=(jax...  52 us
    pallas_call x1, Pallas kernels, finish(): pl.pallas_call(finish_kernel, out_shape=(jax.ShapeDtypeStruct(moved.shape...  1.35 us

profile of v1, /device:TPU:0, one launch (start us, length us, event | category | flops | bytes accessed | tf_op | source)
XLA Modules:
  0.0 54.0 jit_solution(1261113763018666125)
XLA Ops:
  0.6 0.0 copy-start
  0.6 52.0 %shard_map.95 = (f32[2,1024]{1,0:T(2,128)S(1)}, bf16[4,256,512]{2,1,0:T(8,128)(2,1)S(1)}) custom-call(s32[4,1024]{1,0:T(4,128)} %row_ref.1, s32[4,1024]{1,0:T(4,128)} %col_ref.1, s32[4,1024]{1,0:T(4,128)} %bin_ref.1, bf16[1024]{0:T(1024)(128)(2,1)} %charge_ref.1, f32[2,1024]{1,0:T(2,128)} %momentum.1, bf16[8,256,512]{2,1,0:T(8,128)(2,1)} %old.1, ...), custom_call_target="tpu_custom_call" | custom-call | tf_op jit(solution)/shard_map/pallas_call | solution.py:536
  52.7 0.0 copy-done
  52.7 1.3 %shard_map.96 = (f32[2,1024]{1,0:T(2,128)}, bf16[8,256,512]{2,1,0:T(8,128)(2,1)}) custom-call(f32[2,1024]{1,0:T(2,128)S(1)} %get-tuple-element.4.moved, bf16[4,256,512]{2,1,0:T(8,128)(2,1)S(1)} %get-tuple-element.5.newest, bf16[8,256,512]{2,1,0:T(8,128)(2,1)S(1)} %copy-done), custom_call_target="tpu_custom_call" | custom-call | tf_op jit(solution)/shard_map/pallas_call | solution.py:510
Async XLA Ops:
  0.6 52.0 %copy-start = (bf16[8,256,512]{2,1,0:T(8,128)(2,1)S(1)}, bf16[8,256,512]{2,1,0:T(8,128)(2,1)}, u32[]{:S(2)}) copy-start(bf16[8,256,512]{2,1,0:T(8,128)(2,1)} %old.1) | copy-start | bytes 6291460
